TPU v7x, 32 devices: a whole 2x2x4 slice. The times are simulated.
32 devices in a mesh: patch: 16 (over z, x, core), tp: 2 (over y).
Axes of the slice: x: 2, y: 2, z: 4, core: 2. Of those that a mesh axis runs over, the one named last changes fastest.
Arguments:
- resid_corrupt: bfloat16 [512, 4096], P(None, 'tp'), may hold values from -6 to 6
- resid_clean: bfloat16 [2, 512, 4096], P(None, 'patch', 'tp'), may hold values from -6 to 6
- patch_level: int32 [16], P('patch'), may hold values from 0 to 1
- patch_mask: int32 [16, 128], P('patch'), may hold values 0 or 1
- norm_gain: bfloat16 [4096], P('tp'), may hold values from 0.099609375 to 1.8984375
- final_gain: bfloat16 [4096], P('tp'), may hold values from 0.099609375 to 1.8984375
- w_query: bfloat16 [4096, 4096], P('patch', 'tp'), may hold values from -1 to 1
- w_key: bfloat16 [4096, 1024], P('patch', 'tp'), may hold values from -1 to 1
- w_value: bfloat16 [4096, 1024], P('patch', 'tp'), may hold values from -0.09375 to 0.09375
- w_out: bfloat16 [4096, 4096], P('tp', 'patch'), may hold values from -0.09375 to 0.09375
- unembed: bfloat16 [128256, 4096], P(('patch', 'tp')), may hold values from -0.09375 to 0.09375
- scored_ids: int32 [256], replicated, may hold values from 0 to 128255
- base_logits: float32 [512, 256], P('tp'), may hold values from -6 to 6
Outputs:
- logit_shift: float32 [16, 512, 256], P('patch', 'tp')
All inputs are finite; a program needn't handle non-finite values. No bound on the sum of `patch_mask` on one device may be relied on, other than what follows from the above.
Results may differ from a plain program's by a relative error of at most 0.01.
The roundings to bfloat16 on the way count: a program that leaves them out, or rounds other values in their place, can miss the bound.
Values may be sent and summed in bfloat16 or wider, within the bound.
No kernel may reach another device: no remote copies, remote signals or barrier semaphores. Data moves between devices by JAX's collectives and lax.ppermute only.
A program may use at most 192 MiB of HBM per device.

v0:
```python
import jax
import jax.numpy as jnp
from jax import lax
from jax.sharding import PartitionSpec as P

D = 4096
HD = 128
SEQ = 128
PROMPTS = 4
EPSILON = 1e-05
THETA = 500000.0


def rope_tables(length, head_dim):
    half = head_dim // 2
    freqs = THETA ** (-(jnp.arange(half, dtype=jnp.float32) * 2.0 / head_dim))
    angles = jnp.arange(length, dtype=jnp.float32)[:, None] * freqs[None, :]
    return (jnp.cos(angles)[:, None, :], jnp.sin(angles)[:, None, :])


def rotate(values, cosine, sine):
    half = values.shape[-1] // 2
    lower = values[..., :half]
    upper = values[..., half:]
    return jnp.concatenate([lower * cosine - upper * sine, upper * cosine + lower * sine], axis=-1)


def rms_scale(rows, gain):
    return rows * lax.rsqrt(jnp.mean(rows * rows, axis=-1, keepdims=True) + EPSILON) * gain


def attend(query_f, key_f, value_f):
    heads = query_f.shape[1] // HD
    kv_heads = key_f.shape[1] // HD
    group = heads // kv_heads
    prompts = query_f.shape[0] // SEQ
    cosine, sine = rope_tables(SEQ, HD)
    queries = rotate(query_f.reshape(prompts, SEQ, heads, HD), cosine, sine).astype(jnp.bfloat16)
    queries = queries.reshape(prompts, SEQ, kv_heads, group, HD)
    key_rows = rotate(key_f.reshape(prompts, SEQ, kv_heads, HD), cosine, sine).astype(jnp.bfloat16)
    value_rows = value_f.astype(jnp.bfloat16).reshape(prompts, SEQ, kv_heads, HD)
    scores = jnp.einsum(
        "pqkgd,pskd->pkgqs", queries, key_rows, preferred_element_type=jnp.float32
    ) * HD ** (-0.5)
    causal = lax.iota(jnp.int32, SEQ)[:, None] >= lax.iota(jnp.int32, SEQ)[None, :]
    scores = jnp.where(causal, scores, -1e30)
    probs = jax.nn.softmax(scores, axis=-1).astype(jnp.bfloat16)
    attended = jnp.einsum(
        "pkgqs,pskd->pqkgd", probs, value_rows, preferred_element_type=jnp.float32
    )
    return attended.astype(jnp.bfloat16).reshape(prompts * SEQ, heads * HD)


def on_device(
    resid_corrupt,
    resid_clean,
    patch_level,
    patch_mask,
    norm_gain,
    final_gain,
    w_query,
    w_key,
    w_value,
    w_out,
    unembed,
    scored_ids,
    base_logits,
):
    level = patch_level[0]
    row_mask = jnp.tile(patch_mask[0], PROMPTS) == 1
    clean_all = lax.all_gather(resid_clean, "patch", axis=1, tiled=True)
    early = (row_mask & (level == 0))[:, None]
    layer_in = jnp.where(early, clean_all[0], resid_corrupt)
    full_rows, full_gain = (
        lax.all_gather(layer_in, "tp", axis=1, tiled=True),
        lax.all_gather(norm_gain, "tp", axis=0, tiled=True),
    )
    normed = rms_scale(full_rows.astype(jnp.float32), full_gain.astype(jnp.float32)).astype(
        jnp.bfloat16
    )
    query_f = jnp.dot(
        normed,
        lax.all_gather(w_query, "patch", axis=0, tiled=True),
        preferred_element_type=jnp.float32,
    )
    key_f = jnp.dot(
        normed,
        lax.all_gather(w_key, "patch", axis=0, tiled=True),
        preferred_element_type=jnp.float32,
    )
    value_f = jnp.dot(
        normed,
        lax.all_gather(w_value, "patch", axis=0, tiled=True),
        preferred_element_type=jnp.float32,
    )
    attended = attend(query_f, key_f, value_f)
    partial_out = jnp.dot(
        attended,
        lax.all_gather(w_out, "patch", axis=1, tiled=True),
        preferred_element_type=jnp.float32,
    )
    head_block = lax.psum_scatter(
        partial_out.astype(jnp.bfloat16), "tp", scatter_dimension=1, tiled=True
    ).astype(jnp.float32)
    middle = layer_in.astype(jnp.float32) + head_block
    late = (row_mask & (level == 1))[:, None]
    residual = jnp.where(late, clean_all[1].astype(jnp.float32), middle)
    squares = lax.psum(jnp.sum(residual * residual, axis=1), "tp")
    scaling = lax.rsqrt(squares / D + EPSILON)[:, None]
    final_block = (residual * scaling * final_gain.astype(jnp.float32)).astype(jnp.bfloat16)
    rows_dev = unembed.shape[0]
    first_row = lax.axis_index(("patch", "tp")) * rows_dev
    owned_rows = (scored_ids[:, None] == first_row + lax.iota(jnp.int32, rows_dev)[None, :]).astype(
        jnp.bfloat16
    )
    picked = jnp.dot(owned_rows, unembed, preferred_element_type=jnp.float32)
    tp_count = lax.axis_size("tp")
    patch_count = lax.axis_size("patch")
    fine = picked.shape[1] // (tp_count * patch_count)
    reordered = (
        picked.reshape(picked.shape[0], tp_count, patch_count, fine)
        .transpose(0, 2, 1, 3)
        .reshape(picked.shape)
    )
    small_block = lax.psum_scatter(
        reordered, ("patch", "tp"), scatter_dimension=1, tiled=True
    ).astype(jnp.bfloat16)
    score_block = lax.all_gather(small_block, "patch", axis=1, tiled=True)
    partial_logits = jnp.einsum(
        "td,sd->ts", final_block, score_block, preferred_element_type=jnp.float32
    )
    token_logits = lax.psum_scatter(
        partial_logits.astype(jnp.bfloat16), "tp", scatter_dimension=0, tiled=True
    ).astype(jnp.float32)
    return (token_logits - base_logits)[None]


def solution(mesh):
    placed = (
        P(None, "tp"),
        P(None, "patch", "tp"),
        P("patch"),
        P("patch", None),
        P("tp"),
        P("tp"),
        P("patch", "tp"),
        P("patch", "tp"),
        P("patch", "tp"),
        P("tp", "patch"),
        P(("patch", "tp"), None),
        P(),
        P("tp", None),
    )
    return jax.shard_map(
        on_device, mesh=mesh, in_specs=placed, out_specs=P("patch", "tp", None), check_vma=False
    )
```

profile of v0, /device:TPU:0, one launch (start us, length us, event | category | flops | bytes accessed | tf_op | source)
XLA Modules:
  0.0 590.9 jit_solution(3433923609739333319)
XLA Ops:
  7.4 0.7 all-gather.8.cloned.1.call-update
  8.8 0.7 and_bitcast_fusion.1
  9.5 54.0 %all-gather.8.cloned.1.call-done = bf16[2,512,2048]{2,1,0:T(8,128)(2,1)} async-done(((bf16[2,32,2048]{2,1,0:T(8,128)(2,1)}), bf16[2,512,2048]{2,1,0:T(8,128)(2,1)}) %all-gather.8.cloned.1.call-update) | async-done | bytes 4194320 | tf_op jit(solution)/shard_map/all_gather | solution.py:71
  63.5 3.9 fusion.11
  67.4 0.0 all-gather.14.cloned.1.call-start
  67.5 0.7 all-gather.14.cloned.1.call-update
  68.2 0.5 all-gather.12.cloned.1.call-update
  68.8 0.5 all-gather.16.cloned.1.call-update
  69.4 0.5 all-gather.18.cloned.1.call-update
  69.9 0.0 reduce-scatter.6.cloned.1.call-start
  70.0 17.1 %fusion.7 = f32[32,8,32,128]{3,1,2,0:T(8,128)S(1)} fusion(bf16[4008,4096]{1,0:T(8,128)(2,1)} %param.23, s32[4008]{0:T(1024)S(1)} %iota_add_fusion, s32[256]{0:T(256)S(1)} %copy-done.4), kind=kOutput, calls=%fused_computation.18 | convolution fusion | flops 8406411264 | bytes 37044896 | tf_op jit(solution)/shard_map/dot_general | solution.py:116
  87.1 2.7 copy.44
  89.8 5.3 copy.35
  95.1 0.0 reduce-scatter.4.cloned.1.call-start
  95.2 0.6 copy-done.2
  95.8 4.7 all_gather.26
  100.5 0.3 fusion.30
  100.8 23.2 %all-gather.10.cloned.1.call-done = bf16[512,4096]{1,0:T(8,128)(2,1)} async-done(((bf16[512,2048]{1,0:T(8,128)(2,1)}), bf16[512,4096]{1,0:T(8,128)(2,1)}) %all-gather.10.cloned.1.call-update) | async-done | bytes 4194320 | tf_op jit(solution)/shard_map/all_gather | solution.py:75
  123.9 3.1 fusion.1
  127.0 50.4 %all-gather.14.cloned.1.call-done = bf16[4096,512]{1,0:T(8,128)(2,1)} async-done(((bf16[256,512]{1,0:T(8,128)(2,1)}), bf16[4096,512]{1,0:T(8,128)(2,1)}) %all-gather.14.cloned.1.call-update) | async-done | bytes 4194320 | tf_op jit(solution)/shard_map/all_gather | solution.py:88
  177.5 5.8 fusion.35
  183.3 0.4 reshape.117
  183.7 0.6 fusion.38
  184.3 45.9 %all-gather.12.cloned.1.call-done = bf16[4096,512]{1,0:T(8,128)(2,1)} async-done(((bf16[256,512]{1,0:T(8,128)(2,1)}), bf16[4096,512]{1,0:T(8,128)(2,1)}) %all-gather.12.cloned.1.call-update) | async-done | bytes 4194320 | tf_op jit(solution)/shard_map/all_gather | solution.py:93
  230.2 6.6 %convolution_convert_fusion.1 = bf16[512,512]{1,0:T(8,128)(2,1)} fusion(bf16[4096,512]{1,0:T(8,128)(2,1)} %all-gather.12.cloned.1.call-done, bf16[512,4096]{1,0:T(8,128)(2,1)} %all-gather.10.cloned.1.call-done, f32[4096]{0:T(1024)S(1)} %convert_element_type.59, f32[512]{0:T(512)S(1)} %add_rsqrt_fusion.1), kind=kOutput, calls=%fused_computation.38 | convolution fusion | flops 2156134400 | bytes 8931328 | tf_op jit(solution)/shard_map/dot_general | solution.py:91
  236.8 0.3 subtract_convert_fusion.1
  237.1 1.2 reshape.116
  238.3 120.7 %all-gather.16.cloned.1.call-done = bf16[4096,2048]{1,0:T(8,128)(2,1)} async-done(((bf16[256,2048]{1,0:T(8,128)(2,1)}), bf16[4096,2048]{1,0:T(8,128)(2,1)}) %all-gather.16.cloned.1.call-update) | async-done | bytes 16777232 | tf_op jit(solution)/shard_map/all_gather | solution.py:83
  359.0 13.3 %convolution_bitcast_fusion = f32[64,8,16,128]{3,1,2,0:T(8,128)S(1)} fusion(bf16[4096,2048]{1,0:T(8,128)(2,1)} %all-gather.16.cloned.1.call-done, bf16[512,4096]{1,0:T(8,128)(2,1)} %all-gather.10.cloned.1.call-done, f32[4096]{0:T(1024)S(1)} %convert_element_type.59, f32[512]{0:T(512)S(1)} %add_rsqrt_fusion.1), kind=kOutput, calls=%fused_computation.19 | convolution fusion | flops 8598323200 | bytes 25184256 | tf_op jit(solution)/shard_map/dot_general | solution.py:81
  372.3 0.9 copy.43
  373.2 1.4 subtract_convert_fusion
  374.6 0.5 copy.31
  375.2 0.5 copy.30
  375.7 1.6 fusion.12
  377.3 1.1 fusion.39
  378.4 2.1 convert_bitcast_fusion
  380.5 3.4 copy.34
  384.0 2.8 reshape.119
  386.8 103.3 %all-gather.18.cloned.1.call-done = bf16[2048,4096]{1,0:T(8,128)(2,1)} async-done(((bf16[2048,256]{1,0:T(8,128)(2,1)}), bf16[2048,4096]{1,0:T(8,128)(2,1)}) %all-gather.18.cloned.1.call-update) | async-done | bytes 16777232 | tf_op jit(solution)/shard_map/all_gather | solution.py:99
  490.1 14.3 %convolution_convert_fusion = bf16[512,4096]{1,0:T(8,128)(2,1)} fusion(bf16[512,2048]{1,0:T(8,128)(2,1)} %reshape.119, bf16[2048,4096]{1,0:T(8,128)(2,1)} %all-gather.18.cloned.1.call-done), kind=kOutput, calls=%fused_computation.6 | convolution fusion | flops 8592031744 | bytes 23068672 | tf_op jit(solution)/shard_map/dot_general | solution.py:97
  504.6 1.7 convert_element_type.69
  506.3 0.0 reduce-scatter.8.cloned.1.call-start
  506.4 50.7 %reduce-scatter.4.cloned.1.call-done = bf16[512,2048]{1,0:T(8,128)(2,1)} async-done(((bf16[512,4096]{1,0:T(8,128)(2,1)}), bf16[512,2048]{1,0:T(8,128)(2,1)}) %reduce-scatter.4.cloned.1.call-update) | async-done | bytes 2097168 | tf_op jit(solution)/shard_map/reduce_scatter | solution.py:102
  557.1 3.3 multiply_reduce_fusion
  560.4 4.9 psum.7
  565.3 4.5 fusion.25
  569.8 11.8 %reduce-scatter.8.cloned.1.call-done = bf16[256,256]{1,0:T(8,128)(2,1)} async-done(((bf16[512,256]{1,0:T(8,128)(2,1)}), bf16[256,256]{1,0:T(8,128)(2,1)}) %reduce-scatter.8.cloned.1.call-update) | async-done | bytes 131088 | tf_op jit(solution)/shard_map/reduce_scatter | solution.py:132
  581.7 1.6 subtract_bitcast_fusion
  (31 shorter events, 0.4 us)
Async XLA Ops:
  7.4 56.1 %all-gather.8.cloned.1.call-start = ((), (), s32[]{:S(2)}) async-start(), calls=%async_computation.3 | async-start | bytes 4456448 | tf_op jit(solution)/shard_map/all_gather | solution.py:71
  8.1 115.9 %all-gather.10.cloned.1.call-start = ((), (), s32[]{:S(2)}) async-start(), calls=%async_computation.4 | async-start | bytes 6291456 | tf_op jit(solution)/shard_map/all_gather | solution.py:75
  9.5 60.5 %copy-start.4 = (s32[256]{0:T(256)S(1)}, s32[256]{0:T(256)}, u32[]{:S(2)}) copy-start(s32[256]{0:T(256)} %param.24) | copy-start | bytes 3076
  67.4 110.0 %all-gather.14.cloned.1.call-start = ((), (), s32[]{:S(2)}) async-start(), calls=%async_computation.6 | async-start | bytes 4456448 | tf_op jit(solution)/shard_map/all_gather | solution.py:88
  68.2 162.0 %all-gather.12.cloned.1.call-start = ((), (), s32[]{:S(2)}) async-start(), calls=%async_computation.5 | async-start | bytes 4456448 | tf_op jit(solution)/shard_map/all_gather | solution.py:93
  68.7 290.2 %all-gather.16.cloned.1.call-start = ((), (), s32[]{:S(2)}) async-start(), calls=%async_computation.7 | async-start | bytes 17825792 | tf_op jit(solution)/shard_map/all_gather | solution.py:83
  69.3 420.8 %all-gather.18.cloned.1.call-start = ((), (), s32[]{:S(2)}) async-start(), calls=%async_computation.8 | async-start | bytes 17825792 | tf_op jit(solution)/shard_map/all_gather | solution.py:99
  69.9 434.7 %reduce-scatter.6.cloned.1.call-start = ((), (), s32[]{:S(2)}) async-start(), calls=%async_computation.10 | async-start | bytes 4325376 | tf_op jit(solution)/shard_map/reduce_scatter | solution.py:125
  95.1 0.7 copy-start.2
  95.1 462.0 %reduce-scatter.4.cloned.1.call-start = ((), (), s32[]{:S(2)}) async-start(), calls=%async_computation.9 | async-start | bytes 6291456 | tf_op jit(solution)/shard_map/reduce_scatter | solution.py:102
  504.5 1.9 copy-start.3
  504.5 52.6 %copy-start = (bf16[512,2048]{1,0:T(8,128)(2,1)S(1)}, bf16[512,2048]{1,0:T(8,128)(2,1)}, u32[]{:S(2)}) copy-start(bf16[512,2048]{1,0:T(8,128)(2,1)} %fusion.11) | copy-start | bytes 6291460
  504.5 60.8 %all-gather.20.cloned.1.call-start = ((), (), s32[]{:S(2)}) async-start(), calls=%async_computation.11 | async-start | bytes 1114112 | tf_op jit(solution)/shard_map/all_gather | solution.py:128
  506.3 75.4 %reduce-scatter.8.cloned.1.call-start = ((), (), s32[]{:S(2)}) async-start(), calls=%async_computation.12 | async-start | bytes 393216 | tf_op jit(solution)/shard_map/reduce_scatter | solution.py:132
  565.3 16.4 %copy-start.1 = (f32[256,256]{1,0:T(8,128)S(1)}, f32[256,256]{1,0:T(8,128)}, u32[]{:S(2)}) copy-start(f32[256,256]{1,0:T(8,128)} %param.25) | copy-start | bytes 786436
Sparse Core Ops, SparseCore 0:
  10.3 53.1 all-gather.7
  67.5 56.3 all-gather.9
  126.1 51.2 all-gather.13
  179.5 50.6 all-gather.11
  232.2 126.7 all-gather.15
  361.0 129.1 all-gather.17
  507.5 36.0 all-gather.19
Sparse Core Ops, SparseCore 1:
  95.2 264.9 reduce-scatter.5
  504.6 52.5 reduce-scatter.3
  569.9 11.7 reduce-scatter.7
where the time goes:
time: 591 us
  waiting for transfers between devices  463 us (78%)
  matrix products  65.4 us (11%)
  local copies, waits for them, and re-layouts  19 us (3%)
  other arithmetic  17.4 us (3%)
  between operations  15.9 us (3%)
  blocking collectives  9.67 us (2%)
    all_gather x1, waiting for transfers between devices, on_device(): lax.all_gather(w_query, 'patch', axis=0, tiled=True)  121 us
    all_gather x1, waiting for transfers between devices, on_device(): lax.all_gather(w_out, 'patch', axis=1, tiled=True)  103 us
    all_gather x1, waiting for transfers between devices, on_device(): clean_all = lax.all_gather(resid_clean, 'patch', axis=1, tiled=True)  54 us
    reduce_scatter x1, waiting for transfers between devices, on_device(): lax.psum_scatter(partial_out.astype(jnp.bfloat16), 'tp', scatter_dimensio...  50.7 us
    all_gather x1, waiting for transfers between devices, on_device(): lax.all_gather(w_key, 'patch', axis=0, tiled=True)  50.4 us
    all_gather x1, waiting for transfers between devices, on_device(): lax.all_gather(w_value, 'patch', axis=0, tiled=True)  45.9 us
    all_gather x1, waiting for transfers between devices, on_device(): lax.all_gather(layer_in, 'tp', axis=1, tiled=True)  23.2 us
    dot_general x1, matrix products, on_device(): picked = jnp.dot(owned_rows, unembed, preferred_element_type=jnp.float32)  17.1 us
  transfers between devices with their start and end apart: 10, of which 8 were waited for; matrix products, arithmetic and copies ran while one was open for 15% of the time, Pallas kernels for 0%

commit v1 on v0

--- a/solution.py
+++ b/solution.py
@@ -68,7 +68,14 @@
 ):
     level = patch_level[0]
     row_mask = jnp.tile(patch_mask[0], PROMPTS) == 1
-    clean_all = lax.all_gather(resid_clean, "patch", axis=1, tiled=True)
+    ring = [resid_clean]
+    for hop in range(15):
+        ring.append(lax.ppermute(ring[-1], "patch", [(dev, (dev + 1) % 16) for dev in range(16)]))
+    clean_all = jnp.roll(
+        jnp.concatenate(ring[::-1], axis=1),
+        (lax.axis_index("patch") + 1) * ring[0].shape[1],
+        axis=1,
+    )
     early = (row_mask & (level == 0))[:, None]
     layer_in = jnp.where(early, clean_all[0], resid_corrupt)
     full_rows, full_gain = (

time: 591 us -> 673 us (1.14)
  waiting for transfers between devices: 463 us -> 536 us
  local copies, waits for them, and re-layouts: 19 us -> 28.6 us
    ppermute x0 -> x15, waiting for transfers between devices: none -> 127 us  [on_device(): lax.ppermute(ring[-1], 'patch', [(dev, (dev + 1) % 16) for dev in range(1...]
    all_gather x1 -> x0, waiting for transfers between devices: 54 us -> none  [on_device(): clean_all = lax.all_gather(resid_clean, 'patch', axis=1, tiled=True)]
    unnamed x12 -> x53, local copies, waits for them, and re-layouts: 4.22 us -> 13.9 us
  transfers between devices with their start and end apart: 10 -> 24, of which waited for: 8 -> 22; matrix products, arithmetic and copies ran while one was open for 15% -> 14% of each run, Pallas kernels for 0% -> 0%
where the time goes in v1:
time: 673 us; the launch traced here: 672 us
  waiting for transfers between devices  536 us (80%)
  matrix products  65.5 us (10%)
  local copies, waits for them, and re-layouts  28.6 us (4%)
  between operations  16.2 us (2%)
  other arithmetic  15.2 us (2%)
  blocking collectives  9.68 us (1%)
    ppermute x15, waiting for transfers between devices, on_device(): lax.ppermute(ring[-1], 'patch', [(dev, (dev + 1) % 16) for dev in range(1...  127 us
    all_gather x1, waiting for transfers between devices, on_device(): lax.all_gather(w_query, 'patch', axis=0, tiled=True)  121 us
    all_gather x1, waiting for transfers between devices, on_device(): lax.all_gather(w_out, 'patch', axis=1, tiled=True)  103 us
    reduce_scatter x1, waiting for transfers between devices, on_device(): lax.psum_scatter(partial_out.astype(jnp.bfloat16), 'tp', scatter_dimensio...  50.8 us
    all_gather x1, waiting for transfers between devices, on_device(): lax.all_gather(w_key, 'patch', axis=0, tiled=True)  50.5 us
    all_gather x1, waiting for transfers between devices, on_device(): lax.all_gather(w_value, 'patch', axis=0, tiled=True)  46.2 us
    all_gather x1, waiting for transfers between devices, on_device(): lax.all_gather(layer_in, 'tp', axis=1, tiled=True)  22.8 us
    dot_general x1, matrix products, on_device(): picked = jnp.dot(owned_rows, unembed, preferred_element_type=jnp.float32)  17.1 us
  transfers between devices with their start and end apart: 24, of which 22 were waited for; matrix products, arithmetic and copies ran while one was open for 14% of the time, Pallas kernels for 0%

profile of v1, /device:TPU:0, one launch (start us, length us, event | category | flops | bytes accessed | tf_op | source)
XLA Modules:
  0.0 671.9 jit_solution(3826801778822679739)
XLA Ops:
  7.9 9.3 %collective-permute-done = bf16[2,32,2048]{2,1,0:T(8,128)(2,1)S(1)} collective-permute-done((bf16[2,32,2048]{2,1,0:T(8,128)(2,1)}, bf16[2,32,2048]{2,1,0:T(8,128)(2,1)S(1)}, u32[]{:S(2)}, u32[]{:S(2)}) %collective-permute-start) | collective-permute-done | bytes 262176 | tf_op jit(solution)/shard_map/ppermute | solution.py:73
  17.2 8.5 %collective-permute-done.1 = bf16[2,32,2048]{2,1,0:T(8,128)(2,1)S(1)} collective-permute-done((bf16[2,32,2048]{2,1,0:T(8,128)(2,1)S(1)}, bf16[2,32,2048]{2,1,0:T(8,128)(2,1)S(1)}, u32[]{:S(2)}, u32[]{:S(2)}) %collective-permute-start.1) | collective-permute-done | bytes 262176 | tf_op jit(solution)/shard_map/ppermute | solution.py:73
  25.6 8.5 %collective-permute-done.2 = bf16[2,32,2048]{2,1,0:T(8,128)(2,1)S(1)} collective-permute-done((bf16[2,32,2048]{2,1,0:T(8,128)(2,1)S(1)}, bf16[2,32,2048]{2,1,0:T(8,128)(2,1)S(1)}, u32[]{:S(2)}, u32[]{:S(2)}) %collective-permute-start.2) | collective-permute-done | bytes 262176 | tf_op jit(solution)/shard_map/ppermute | solution.py:73
  34.1 8.5 %collective-permute-done.3 = bf16[2,32,2048]{2,1,0:T(8,128)(2,1)S(1)} collective-permute-done((bf16[2,32,2048]{2,1,0:T(8,128)(2,1)S(1)}, bf16[2,32,2048]{2,1,0:T(8,128)(2,1)S(1)}, u32[]{:S(2)}, u32[]{:S(2)}) %collective-permute-start.3) | collective-permute-done | bytes 262176 | tf_op jit(solution)/shard_map/ppermute | solution.py:73
  42.6 8.5 %collective-permute-done.4 = bf16[2,32,2048]{2,1,0:T(8,128)(2,1)S(1)} collective-permute-done((bf16[2,32,2048]{2,1,0:T(8,128)(2,1)S(1)}, bf16[2,32,2048]{2,1,0:T(8,128)(2,1)S(1)}, u32[]{:S(2)}, u32[]{:S(2)}) %collective-permute-start.4) | collective-permute-done | bytes 262176 | tf_op jit(solution)/shard_map/ppermute | solution.py:73
  51.1 8.5 %collective-permute-done.5 = bf16[2,32,2048]{2,1,0:T(8,128)(2,1)S(1)} collective-permute-done((bf16[2,32,2048]{2,1,0:T(8,128)(2,1)S(1)}, bf16[2,32,2048]{2,1,0:T(8,128)(2,1)S(1)}, u32[]{:S(2)}, u32[]{:S(2)}) %collective-permute-start.5) | collective-permute-done | bytes 262176 | tf_op jit(solution)/shard_map/ppermute | solution.py:73
  59.6 8.5 %collective-permute-done.6 = bf16[2,32,2048]{2,1,0:T(8,128)(2,1)S(1)} collective-permute-done((bf16[2,32,2048]{2,1,0:T(8,128)(2,1)S(1)}, bf16[2,32,2048]{2,1,0:T(8,128)(2,1)S(1)}, u32[]{:S(2)}, u32[]{:S(2)}) %collective-permute-start.6) | collective-permute-done | bytes 262176 | tf_op jit(solution)/shard_map/ppermute | solution.py:73
  68.1 8.5 %collective-permute-done.7 = bf16[2,32,2048]{2,1,0:T(8,128)(2,1)S(1)} collective-permute-done((bf16[2,32,2048]{2,1,0:T(8,128)(2,1)S(1)}, bf16[2,32,2048]{2,1,0:T(8,128)(2,1)S(1)}, u32[]{:S(2)}, u32[]{:S(2)}) %collective-permute-start.7) | collective-permute-done | bytes 262176 | tf_op jit(solution)/shard_map/ppermute | solution.py:73
  76.6 8.5 %collective-permute-done.8 = bf16[2,32,2048]{2,1,0:T(8,128)(2,1)S(1)} collective-permute-done((bf16[2,32,2048]{2,1,0:T(8,128)(2,1)S(1)}, bf16[2,32,2048]{2,1,0:T(8,128)(2,1)S(1)}, u32[]{:S(2)}, u32[]{:S(2)}) %collective-permute-start.8) | collective-permute-done | bytes 262176 | tf_op jit(solution)/shard_map/ppermute | solution.py:73
  85.1 8.5 %collective-permute-done.9 = bf16[2,32,2048]{2,1,0:T(8,128)(2,1)S(1)} collective-permute-done((bf16[2,32,2048]{2,1,0:T(8,128)(2,1)S(1)}, bf16[2,32,2048]{2,1,0:T(8,128)(2,1)S(1)}, u32[]{:S(2)}, u32[]{:S(2)}) %collective-permute-start.9) | collective-permute-done | bytes 262176 | tf_op jit(solution)/shard_map/ppermute | solution.py:73
  93.6 8.5 %collective-permute-done.10 = bf16[2,32,2048]{2,1,0:T(8,128)(2,1)S(1)} collective-permute-done((bf16[2,32,2048]{2,1,0:T(8,128)(2,1)S(1)}, bf16[2,32,2048]{2,1,0:T(8,128)(2,1)S(1)}, u32[]{:S(2)}, u32[]{:S(2)}) %collective-permute-start.10) | collective-permute-done | bytes 262176 | tf_op jit(solution)/shard_map/ppermute | solution.py:73
  102.1 8.5 %collective-permute-done.11 = bf16[2,32,2048]{2,1,0:T(8,128)(2,1)S(1)} collective-permute-done((bf16[2,32,2048]{2,1,0:T(8,128)(2,1)S(1)}, bf16[2,32,2048]{2,1,0:T(8,128)(2,1)S(1)}, u32[]{:S(2)}, u32[]{:S(2)}) %collective-permute-start.11) | collective-permute-done | bytes 262176 | tf_op jit(solution)/shard_map/ppermute | solution.py:73
  110.6 8.5 %collective-permute-done.12 = bf16[2,32,2048]{2,1,0:T(8,128)(2,1)S(1)} collective-permute-done((bf16[2,32,2048]{2,1,0:T(8,128)(2,1)S(1)}, bf16[2,32,2048]{2,1,0:T(8,128)(2,1)S(1)}, u32[]{:S(2)}, u32[]{:S(2)}) %collective-permute-start.12) | collective-permute-done | bytes 262176 | tf_op jit(solution)/shard_map/ppermute | solution.py:73
  120.4 7.9 %collective-permute-done.13 = bf16[2,32,2048]{2,1,0:T(8,128)(2,1)} collective-permute-done((bf16[2,32,2048]{2,1,0:T(8,128)(2,1)S(1)}, bf16[2,32,2048]{2,1,0:T(8,128)(2,1)}, u32[]{:S(2)}, u32[]{:S(2)}) %collective-permute-start.13) | collective-permute-done | bytes 262176 | tf_op jit(solution)/shard_map/ppermute | solution.py:73
  129.1 8.1 %collective-permute-done.14 = bf16[2,32,2048]{2,1,0:T(8,128)(2,1)} collective-permute-done((bf16[2,32,2048]{2,1,0:T(8,128)(2,1)}, bf16[2,32,2048]{2,1,0:T(8,128)(2,1)}, u32[]{:S(2)}, u32[]{:S(2)}) %collective-permute-start.14) | collective-permute-done | bytes 262176 | tf_op jit(solution)/shard_map/ppermute | solution.py:73
  138.2 1.0 constant_dynamic-update-slice_fusion.30
  139.1 1.0 constant_dynamic-update-slice_fusion.29
  140.4 1.0 constant_dynamic-update-slice_fusion.16
  143.8 3.2 copy-done.1
  147.0 1.9 fusion.11
  151.7 17.1 %fusion.7 = f32[32,8,32,128]{3,1,2,0:T(8,128)S(1)} fusion(bf16[4008,4096]{1,0:T(8,128)(2,1)} %param.23, s32[4008]{0:T(1024)S(1)} %iota_add_fusion, s32[256]{0:T(256)S(1)} %copy-done.9), kind=kOutput, calls=%fused_computation.18 | convolution fusion | flops 8406411264 | bytes 37044896 | tf_op jit(solution)/shard_map/dot_general | solution.py:123
  168.8 2.7 copy.44
  171.5 5.2 copy.35
  176.8 4.7 all_gather.22
  181.9 22.8 %all-gather.7.cloned.1.call-done = bf16[512,4096]{1,0:T(8,128)(2,1)} async-done(((bf16[512,2048]{1,0:T(8,128)(2,1)}), bf16[512,4096]{1,0:T(8,128)(2,1)}) %all-gather.7.cloned.1.call-update) | async-done | bytes 4194320 | tf_op jit(solution)/shard_map/all_gather | solution.py:82
  204.7 3.1 fusion.1
  207.8 50.5 %all-gather.11.cloned.1.call-done = bf16[4096,512]{1,0:T(8,128)(2,1)} async-done(((bf16[256,512]{1,0:T(8,128)(2,1)}), bf16[4096,512]{1,0:T(8,128)(2,1)}) %all-gather.11.cloned.1.call-update) | async-done | bytes 4194320 | tf_op jit(solution)/shard_map/all_gather | solution.py:95
  258.3 5.8 fusion.36
  265.1 46.2 %all-gather.9.cloned.1.call-done = bf16[4096,512]{1,0:T(8,128)(2,1)} async-done(((bf16[256,512]{1,0:T(8,128)(2,1)}), bf16[4096,512]{1,0:T(8,128)(2,1)}) %all-gather.9.cloned.1.call-update) | async-done | bytes 4194320 | tf_op jit(solution)/shard_map/all_gather | solution.py:100
  311.4 6.7 convolution_convert_fusion.1
  318.3 1.2 reshape.116
  319.5 120.5 %all-gather.13.cloned.1.call-done = bf16[4096,2048]{1,0:T(8,128)(2,1)} async-done(((bf16[256,2048]{1,0:T(8,128)(2,1)}), bf16[4096,2048]{1,0:T(8,128)(2,1)}) %all-gather.13.cloned.1.call-update) | async-done | bytes 16777232 | tf_op jit(solution)/shard_map/all_gather | solution.py:90
  440.1 13.3 %convolution_bitcast_fusion = f32[64,8,16,128]{3,1,2,0:T(8,128)S(1)} fusion(bf16[4096,2048]{1,0:T(8,128)(2,1)} %all-gather.13.cloned.1.call-done, bf16[512,4096]{1,0:T(8,128)(2,1)} %all-gather.7.cloned.1.call-done, f32[4096]{0:T(1024)S(1)} %convert_element_type.59, f32[512]{0:T(512)S(1)} %add_rsqrt_fusion.1), kind=kOutput, calls=%fused_computation.19 | convolution fusion | flops 8598323200 | bytes 25184256 | tf_op jit(solution)/shard_map/dot_general | solution.py:88
  454.3 1.4 subtract_convert_fusion
  456.8 1.6 fusion.12
  458.4 1.1 fusion.40
  459.5 2.1 convert_bitcast_fusion
  461.6 3.4 copy.34
  465.1 2.8 reshape.119
  467.9 103.2 %all-gather.15.cloned.1.call-done = bf16[2048,4096]{1,0:T(8,128)(2,1)} async-done(((bf16[2048,256]{1,0:T(8,128)(2,1)}), bf16[2048,4096]{1,0:T(8,128)(2,1)}) %all-gather.15.cloned.1.call-update) | async-done | bytes 16777232 | tf_op jit(solution)/shard_map/all_gather | solution.py:106
  571.1 14.4 %convolution_convert_fusion = bf16[512,4096]{1,0:T(8,128)(2,1)} fusion(bf16[512,2048]{1,0:T(8,128)(2,1)} %reshape.119, bf16[2048,4096]{1,0:T(8,128)(2,1)} %all-gather.15.cloned.1.call-done), kind=kOutput, calls=%fused_computation.6 | convolution fusion | flops 8592031744 | bytes 23068672 | tf_op jit(solution)/shard_map/dot_general | solution.py:104
  585.6 1.5 convert_element_type.69
  587.3 50.8 %reduce-scatter.4.cloned.1.call-done = bf16[512,2048]{1,0:T(8,128)(2,1)} async-done(((bf16[512,4096]{1,0:T(8,128)(2,1)}), bf16[512,2048]{1,0:T(8,128)(2,1)}) %reduce-scatter.4.cloned.1.call-update) | async-done | bytes 2097168 | tf_op jit(solution)/shard_map/reduce_scatter | solution.py:109
  638.2 3.3 multiply_reduce_fusion
  641.4 4.9 psum.7
  646.4 4.4 fusion.25
  650.9 11.8 %reduce-scatter.8.cloned.1.call-done = bf16[256,256]{1,0:T(8,128)(2,1)} async-done(((bf16[512,256]{1,0:T(8,128)(2,1)}), bf16[256,256]{1,0:T(8,128)(2,1)}) %reduce-scatter.8.cloned.1.call-update) | async-done | bytes 131088 | tf_op jit(solution)/shard_map/reduce_scatter | solution.py:139
  662.7 1.6 subtract_bitcast_fusion
  (100 shorter events, 11.8 us)
Async XLA Ops:
  7.4 136.4 %copy-start.3 = (bf16[2,32,2048]{2,1,0:T(8,128)(2,1)S(1)}, bf16[2,32,2048]{2,1,0:T(8,128)(2,1)}, u32[]{:S(2)}) copy-start(bf16[2,32,2048]{2,1,0:T(8,128)(2,1)} %param.14) | copy-start | bytes 786436
  7.4 197.3 %all-gather.7.cloned.1.call-start = ((), (), s32[]{:S(2)}) async-start(), calls=%async_computation.3 | async-start | bytes 6291456 | tf_op jit(solution)/shard_map/all_gather | solution.py:82
  7.4 9.8 %collective-permute-start = (bf16[2,32,2048]{2,1,0:T(8,128)(2,1)}, bf16[2,32,2048]{2,1,0:T(8,128)(2,1)S(1)}, u32[]{:S(2)}, u32[]{:S(2)}) collective-permute-start(bf16[2,32,2048]{2,1,0:T(8,128)(2,1)} %param.14), channel_id=1, source_target_pairs={{0,2},{2,4},{4,6},{6,8},{8,10},{10,12},{12,14},{14,16},{16,18},{18... | collective-permute-start | bytes 786440 | tf_op jit(solution)/shard_map/ppermute | solution.py:73
  17.1 8.5 %collective-permute-start.1 = (bf16[2,32,2048]{2,1,0:T(8,128)(2,1)S(1)}, bf16[2,32,2048]{2,1,0:T(8,128)(2,1)S(1)}, u32[]{:S(2)}, u32[]{:S(2)}) collective-permute-start(bf16[2,32,2048]{2,1,0:T(8,128)(2,1)S(1)} %collective-permute-done), channel_id=1, source_target_pairs={{0,2},{2,4},{4,6},{6,8},{8,10},{10,12},{12,14},{14,16},{16,18},{18... | collective-permute-start | bytes 786440 | tf_op jit(solution)/shard_map/ppermute | solution.py:73
  25.6 8.5 %collective-permute-start.2 = (bf16[2,32,2048]{2,1,0:T(8,128)(2,1)S(1)}, bf16[2,32,2048]{2,1,0:T(8,128)(2,1)S(1)}, u32[]{:S(2)}, u32[]{:S(2)}) collective-permute-start(bf16[2,32,2048]{2,1,0:T(8,128)(2,1)S(1)} %collective-permute-done.1), channel_id=1, source_target_pairs={{0,2},{2,4},{4,6},{6,8},{8,10},{10,12},{12,14},{14,16},{16,18},{18... | collective-permute-start | bytes 786440 | tf_op jit(solution)/shard_map/ppermute | solution.py:73
  34.1 8.5 %collective-permute-start.3 = (bf16[2,32,2048]{2,1,0:T(8,128)(2,1)S(1)}, bf16[2,32,2048]{2,1,0:T(8,128)(2,1)S(1)}, u32[]{:S(2)}, u32[]{:S(2)}) collective-permute-start(bf16[2,32,2048]{2,1,0:T(8,128)(2,1)S(1)} %collective-permute-done.2), channel_id=1, source_target_pairs={{0,2},{2,4},{4,6},{6,8},{8,10},{10,12},{12,14},{14,16},{16,18},{18... | collective-permute-start | bytes 786440 | tf_op jit(solution)/shard_map/ppermute | solution.py:73
  42.6 8.5 %collective-permute-start.4 = (bf16[2,32,2048]{2,1,0:T(8,128)(2,1)S(1)}, bf16[2,32,2048]{2,1,0:T(8,128)(2,1)S(1)}, u32[]{:S(2)}, u32[]{:S(2)}) collective-permute-start(bf16[2,32,2048]{2,1,0:T(8,128)(2,1)S(1)} %collective-permute-done.3), channel_id=1, source_target_pairs={{0,2},{2,4},{4,6},{6,8},{8,10},{10,12},{12,14},{14,16},{16,18},{18... | collective-permute-start | bytes 786440 | tf_op jit(solution)/shard_map/ppermute | solution.py:73
  51.1 8.5 %collective-permute-start.5 = (bf16[2,32,2048]{2,1,0:T(8,128)(2,1)S(1)}, bf16[2,32,2048]{2,1,0:T(8,128)(2,1)S(1)}, u32[]{:S(2)}, u32[]{:S(2)}) collective-permute-start(bf16[2,32,2048]{2,1,0:T(8,128)(2,1)S(1)} %collective-permute-done.4), channel_id=1, source_target_pairs={{0,2},{2,4},{4,6},{6,8},{8,10},{10,12},{12,14},{14,16},{16,18},{18... | collective-permute-start | bytes 786440 | tf_op jit(solution)/shard_map/ppermute | solution.py:73
  59.6 8.5 %collective-permute-start.6 = (bf16[2,32,2048]{2,1,0:T(8,128)(2,1)S(1)}, bf16[2,32,2048]{2,1,0:T(8,128)(2,1)S(1)}, u32[]{:S(2)}, u32[]{:S(2)}) collective-permute-start(bf16[2,32,2048]{2,1,0:T(8,128)(2,1)S(1)} %collective-permute-done.5), channel_id=1, source_target_pairs={{0,2},{2,4},{4,6},{6,8},{8,10},{10,12},{12,14},{14,16},{16,18},{18... | collective-permute-start | bytes 786440 | tf_op jit(solution)/shard_map/ppermute | solution.py:73
  68.1 8.5 %collective-permute-start.7 = (bf16[2,32,2048]{2,1,0:T(8,128)(2,1)S(1)}, bf16[2,32,2048]{2,1,0:T(8,128)(2,1)S(1)}, u32[]{:S(2)}, u32[]{:S(2)}) collective-permute-start(bf16[2,32,2048]{2,1,0:T(8,128)(2,1)S(1)} %collective-permute-done.6), channel_id=1, source_target_pairs={{0,2},{2,4},{4,6},{6,8},{8,10},{10,12},{12,14},{14,16},{16,18},{18... | collective-permute-start | bytes 786440 | tf_op jit(solution)/shard_map/ppermute | solution.py:73
  76.6 8.5 %collective-permute-start.8 = (bf16[2,32,2048]{2,1,0:T(8,128)(2,1)S(1)}, bf16[2,32,2048]{2,1,0:T(8,128)(2,1)S(1)}, u32[]{:S(2)}, u32[]{:S(2)}) collective-permute-start(bf16[2,32,2048]{2,1,0:T(8,128)(2,1)S(1)} %collective-permute-done.7), channel_id=1, source_target_pairs={{0,2},{2,4},{4,6},{6,8},{8,10},{10,12},{12,14},{14,16},{16,18},{18... | collective-permute-start | bytes 786440 | tf_op jit(solution)/shard_map/ppermute | solution.py:73
  85.1 8.5 %collective-permute-start.9 = (bf16[2,32,2048]{2,1,0:T(8,128)(2,1)S(1)}, bf16[2,32,2048]{2,1,0:T(8,128)(2,1)S(1)}, u32[]{:S(2)}, u32[]{:S(2)}) collective-permute-start(bf16[2,32,2048]{2,1,0:T(8,128)(2,1)S(1)} %collective-permute-done.8), channel_id=1, source_target_pairs={{0,2},{2,4},{4,6},{6,8},{8,10},{10,12},{12,14},{14,16},{16,18},{18... | collective-permute-start | bytes 786440 | tf_op jit(solution)/shard_map/ppermute | solution.py:73
  93.6 8.5 %collective-permute-start.10 = (bf16[2,32,2048]{2,1,0:T(8,128)(2,1)S(1)}, bf16[2,32,2048]{2,1,0:T(8,128)(2,1)S(1)}, u32[]{:S(2)}, u32[]{:S(2)}) collective-permute-start(bf16[2,32,2048]{2,1,0:T(8,128)(2,1)S(1)} %collective-permute-done.9), channel_id=1, source_target_pairs={{0,2},{2,4},{4,6},{6,8},{8,10},{10,12},{12,14},{14,16},{16,18},{18... | collective-permute-start | bytes 786440 | tf_op jit(solution)/shard_map/ppermute | solution.py:73
  102.1 8.5 %collective-permute-start.11 = (bf16[2,32,2048]{2,1,0:T(8,128)(2,1)S(1)}, bf16[2,32,2048]{2,1,0:T(8,128)(2,1)S(1)}, u32[]{:S(2)}, u32[]{:S(2)}) collective-permute-start(bf16[2,32,2048]{2,1,0:T(8,128)(2,1)S(1)} %collective-permute-done.10), channel_id=1, source_target_pairs={{0,2},{2,4},{4,6},{6,8},{8,10},{10,12},{12,14},{14,16},{16,18},{18... | collective-permute-start | bytes 786440 | tf_op jit(solution)/shard_map/ppermute | solution.py:73
  110.6 8.5 %collective-permute-start.12 = (bf16[2,32,2048]{2,1,0:T(8,128)(2,1)S(1)}, bf16[2,32,2048]{2,1,0:T(8,128)(2,1)S(1)}, u32[]{:S(2)}, u32[]{:S(2)}) collective-permute-start(bf16[2,32,2048]{2,1,0:T(8,128)(2,1)S(1)} %collective-permute-done.11), channel_id=1, source_target_pairs={{0,2},{2,4},{4,6},{6,8},{8,10},{10,12},{12,14},{14,16},{16,18},{18... | collective-permute-start | bytes 786440 | tf_op jit(solution)/shard_map/ppermute | solution.py:73
  119.1 0.7 copy-start.4
  119.8 8.6 %collective-permute-start.13 = (bf16[2,32,2048]{2,1,0:T(8,128)(2,1)S(1)}, bf16[2,32,2048]{2,1,0:T(8,128)(2,1)}, u32[]{:S(2)}, u32[]{:S(2)}) collective-permute-start(bf16[2,32,2048]{2,1,0:T(8,128)(2,1)S(1)} %collective-permute-done.12), channel_id=1, source_target_pairs={{0,2},{2,4},{4,6},{6,8},{8,10},{10,12},{12,14},{14,16},{16,18},{18... | collective-permute-start | bytes 786440 | tf_op jit(solution)/shard_map/ppermute | solution.py:73
  128.4 8.8 %collective-permute-start.14 = (bf16[2,32,2048]{2,1,0:T(8,128)(2,1)}, bf16[2,32,2048]{2,1,0:T(8,128)(2,1)}, u32[]{:S(2)}, u32[]{:S(2)}) collective-permute-start(bf16[2,32,2048]{2,1,0:T(8,128)(2,1)} %collective-permute-done.13), channel_id=1, source_target_pairs={{0,2},{2,4},{4,6},{6,8},{8,10},{10,12},{12,14},{14,16},{16,18},{18... | collective-permute-start | bytes 786440 | tf_op jit(solution)/shard_map/ppermute | solution.py:73
  129.1 14.3 %copy-start.5 = (bf16[2,32,2048]{2,1,0:T(8,128)(2,1)S(1)}, bf16[2,32,2048]{2,1,0:T(8,128)(2,1)}, u32[]{:S(2)}) copy-start(bf16[2,32,2048]{2,1,0:T(8,128)(2,1)} %copy-done.4) | copy-start | bytes 786436
  129.1 18.0 %copy-start.2 = (bf16[512,2048]{1,0:T(8,128)(2,1)S(1)}, bf16[512,2048]{1,0:T(8,128)(2,1)}, u32[]{:S(2)}) copy-start(bf16[512,2048]{1,0:T(8,128)(2,1)} %param.13) | copy-start | bytes 6291460
  143.5 8.2 %copy-start.9 = (s32[256]{0:T(256)S(1)}, s32[256]{0:T(256)}, u32[]{:S(2)}) copy-start(s32[256]{0:T(256)} %param.24) | copy-start | bytes 3076
  143.8 3.2 copy-start.1
  149.0 109.3 %all-gather.11.cloned.1.call-start = ((), (), s32[]{:S(2)}) async-start(), calls=%async_computation.5 | async-start | bytes 4456448 | tf_op jit(solution)/shard_map/all_gather | solution.py:95
  149.7 161.6 %all-gather.9.cloned.1.call-start = ((), (), s32[]{:S(2)}) async-start(), calls=%async_computation.4 | async-start | bytes 4456448 | tf_op jit(solution)/shard_map/all_gather | solution.py:100
  150.5 289.6 %all-gather.13.cloned.1.call-start = ((), (), s32[]{:S(2)}) async-start(), calls=%async_computation.6 | async-start | bytes 17825792 | tf_op jit(solution)/shard_map/all_gather | solution.py:90
  151.0 420.1 %all-gather.15.cloned.1.call-start = ((), (), s32[]{:S(2)}) async-start(), calls=%async_computation.7 | async-start | bytes 17825792 | tf_op jit(solution)/shard_map/all_gather | solution.py:106
  151.6 434.0 %reduce-scatter.6.cloned.1.call-start = ((), (), s32[]{:S(2)}) async-start(), calls=%async_computation.9 | async-start | bytes 4325376 | tf_op jit(solution)/shard_map/reduce_scatter | solution.py:132
  171.5 5.4 copy-start.7
  176.7 461.4 %reduce-scatter.4.cloned.1.call-start = ((), (), s32[]{:S(2)}) async-start(), calls=%async_computation.8 | async-start | bytes 6291456 | tf_op jit(solution)/shard_map/reduce_scatter | solution.py:109
  467.9 119.4 %copy-start.8 = (bf16[2048]{0:T(1024)(128)(2,1)S(1)}, bf16[2048]{0:T(1024)(128)(2,1)}, u32[]{:S(2)}) copy-start(bf16[2048]{0:T(1024)(128)(2,1)} %param.18) | copy-start | bytes 12292
  467.9 170.3 %copy-start = (bf16[512,2048]{1,0:T(8,128)(2,1)S(1)}, bf16[512,2048]{1,0:T(8,128)(2,1)}, u32[]{:S(2)}) copy-start(bf16[512,2048]{1,0:T(8,128)(2,1)} %fusion.11) | copy-start | bytes 6291460
  585.6 60.8 %all-gather.17.cloned.1.call-start = ((), (), s32[]{:S(2)}) async-start(), calls=%async_computation.10 | async-start | bytes 1114112 | tf_op jit(solution)/shard_map/all_gather | solution.py:135
  587.2 75.5 %reduce-scatter.8.cloned.1.call-start = ((), (), s32[]{:S(2)}) async-start(), calls=%async_computation.11 | async-start | bytes 393216 | tf_op jit(solution)/shard_map/reduce_scatter | solution.py:139
  587.3 75.4 %copy-start.6 = (f32[256,256]{1,0:T(8,128)S(1)}, f32[256,256]{1,0:T(8,128)}, u32[]{:S(2)}) copy-start(f32[256,256]{1,0:T(8,128)} %param.25) | copy-start | bytes 786436
Sparse Core Ops, SparseCore 0:
  149.1 55.5 all-gather.6
  206.8 51.4 all-gather.10
  260.5 50.8 all-gather.8
  313.4 126.6 all-gather.12
  442.1 129.0 all-gather.14
  588.2 36.0 all-gather.16
Sparse Core Ops, SparseCore 1:
  176.8 264.5 reduce-scatter.5
  585.6 52.5 reduce-scatter.3
  650.9 11.7 reduce-scatter.7
